TPU v7x, 32 devices: a whole 2x2x4 slice. The times are simulated.
32 devices in a mesh: row: 4 (over y, x), col: 8 (over z, core).
Axes of the slice: x: 2, y: 2, z: 4, core: 2. Of those that a mesh axis runs over, the one named last changes fastest.
Arguments:
- pair: float32 [256, 256, 128], P('row', 'col'), may hold values from -6 to 6
- valid_length: int32 [1], replicated, may hold values from 64 to 255
- tri_in: bfloat16 [128, 512], replicated, may hold values from -0.5 to 0.5
- tri_gate: bfloat16 [128, 128], replicated, may hold values from -0.5 to 0.5
- tri_out: bfloat16 [128, 128], replicated, may hold values from -0.5 to 0.5
- att_in: bfloat16 [128, 512], replicated, may hold values from -16.9705627 to 16.9705627
- att_bias: bfloat16 [128, 4], replicated, may hold values from -0.5 to 0.5
- att_out: bfloat16 [128, 128], replicated, may hold values from -0.5 to 0.5
Outputs:
- pair_out: float32 [256, 256, 128], P('row', 'col')
Inputs may be any that keep to these rules, and one draw needn't show every extreme that they name: Tokens at positions below valid_length[0] are real, the rest are padding.
All inputs are finite; a program needn't handle non-finite values.
Results may differ from a plain program's by a relative error of at most 0.025.
Values may be sent and summed in bfloat16 or wider, within the bound.
A program may use at most 128 MiB of HBM per device.

v0:
```python
import jax
import jax.numpy as jnp
from jax import lax
from jax.sharding import PartitionSpec as P


def layer_norm(values):
    center = values - jnp.mean(values, axis=-1, keepdims=True)
    return center * lax.rsqrt(jnp.mean(center * center, axis=-1, keepdims=True) + 1e-05)


def fold_keys(carry, keys_piece, values_piece, query_blocks, bias_heads, mask_bias):
    count = keys_piece.shape[1]
    nblocks, brows, cols_dev, heads, head_size = query_blocks.shape
    key_blocks = keys_piece.reshape(nblocks, brows, count, heads, head_size)
    value_blocks = values_piece.reshape(nblocks, brows, count, heads, head_size)

    def one_block(packed):
        query, keys, values, run_max, run_sum, accum = packed
        scores = jnp.einsum("ijhd,ikhd->ihjk", query, keys, preferred_element_type=jnp.float32)
        scores = scores + bias_heads[None] + mask_bias[None, None, None, :]
        new_max = jnp.maximum(run_max, jnp.max(scores, axis=-1))
        factor = jnp.exp(run_max - new_max)
        expo = jnp.exp(scores - new_max[..., None])
        new_sum = run_sum * factor + jnp.sum(expo, axis=-1)
        new_acc = accum * jnp.transpose(factor, (0, 2, 1))[..., None]
        new_acc = new_acc + jnp.einsum("ihjk,ikhd->ijhd", expo, values.astype(jnp.float32))
        return (new_max, new_sum, new_acc)

    return lax.map(one_block, (query_blocks, key_blocks, value_blocks) + tuple(carry))


def per_device(pair, valid_length, tri_in, tri_gate, tri_out, att_in, att_bias, att_out):
    rows_dev, cols_dev, width = pair.shape
    hidden = tri_out.shape[0]
    heads = att_bias.shape[1]
    head_size = width // heads
    total = cols_dev * lax.axis_size("col")
    row_start = lax.axis_index("row") * rows_dev
    col_start = lax.axis_index("col") * cols_dev
    tokens = jnp.arange(total)
    keep_all = (tokens < valid_length[0]).astype(jnp.float32)
    keep_rows = lax.dynamic_slice_in_dim(keep_all, row_start, rows_dev)
    keep_cols = lax.dynamic_slice_in_dim(keep_all, col_start, cols_dev)
    normed_pair = layer_norm(pair).astype(jnp.bfloat16)
    projected = jnp.dot(normed_pair, tri_in, preferred_element_type=jnp.float32)
    weight = (keep_rows[:, None] * keep_cols[None, :])[:, :, None]
    left_edges = (
        jax.nn.sigmoid(projected[..., :hidden]) * projected[..., hidden : 2 * hidden] * weight
    ).astype(jnp.bfloat16)
    right_edges = (
        jax.nn.sigmoid(projected[..., 2 * hidden : 3 * hidden])
        * projected[..., 3 * hidden :]
        * weight
    ).astype(jnp.bfloat16)
    right_rows = lax.all_gather(right_edges, "row", axis=0, tiled=True)
    swapped = lax.psum_scatter(
        jnp.einsum(
            "jkc,ikc->jic", right_rows, left_edges, preferred_element_type=jnp.float32
        ).astype(jnp.bfloat16),
        "col",
        scatter_dimension=0,
        tiled=True,
    ).astype(jnp.float32)
    normed_swapped = layer_norm(swapped).astype(jnp.bfloat16)
    tri_part = jnp.einsum(
        "jic,cd->ijd", normed_swapped, tri_out, preferred_element_type=jnp.float32
    )
    middle = (
        pair
        + jax.nn.sigmoid(jnp.dot(normed_pair, tri_gate, preferred_element_type=jnp.float32))
        * tri_part
    )
    normed_mid = layer_norm(middle).astype(jnp.bfloat16)
    bias_local = jnp.dot(normed_mid, att_bias, preferred_element_type=jnp.float32).astype(
        jnp.bfloat16
    )
    bias_rows = lax.all_gather(bias_local, "row", axis=0, tiled=True)
    bias_cols = lax.all_to_all(bias_rows, "col", split_axis=0, concat_axis=1, tiled=True)
    bias_heads = jnp.transpose(bias_cols.astype(jnp.float32), (2, 0, 1))
    mask_bias = jnp.where(tokens < valid_length[0], 0.0, -1000000000.0).astype(jnp.float32)
    nblocks = rows_dev // 8
    query = (
        jnp.dot(normed_mid, att_in[:, :width], preferred_element_type=jnp.float32)
        * head_size ** (-0.5)
    ).astype(jnp.bfloat16)
    query_blocks = query.reshape(nblocks, 8, cols_dev, heads, head_size)
    gate = jax.nn.sigmoid(
        jnp.dot(normed_mid, att_in[:, 3 * width :], preferred_element_type=jnp.float32)
    )
    start_state = (
        jnp.full((nblocks, 8, heads, cols_dev), -1e30, jnp.float32),
        jnp.zeros((nblocks, 8, heads, cols_dev), jnp.float32),
        jnp.zeros((nblocks, 8, cols_dev, heads, head_size), jnp.float32),
    )
    made = jnp.dot(
        lax.all_gather(normed_mid, "col", axis=1, tiled=True),
        att_in[:, width : 3 * width],
        preferred_element_type=jnp.float32,
    )
    keys_piece = made[..., :width].astype(jnp.bfloat16)
    values_piece = made[..., width:].astype(jnp.bfloat16)
    state = fold_keys(start_state, keys_piece, values_piece, query_blocks, bias_heads, mask_bias)
    run_sum = state[1]
    accum = state[2]
    attended = accum / jnp.transpose(run_sum, (0, 1, 3, 2))[..., None]
    attended = attended.reshape(rows_dev, cols_dev, width)
    gated = (gate * attended).astype(jnp.bfloat16)
    return middle + jnp.dot(gated, att_out, preferred_element_type=jnp.float32)


def solution(mesh):
    placed = (P("row", "col", None), P(), P(), P(), P(), P(), P(), P())
    return jax.shard_map(
        per_device, mesh=mesh, in_specs=placed, out_specs=P("row", "col", None), check_vma=False
    )
```

profile of v0, /device:TPU:0, one launch (start us, length us, event | category | flops | bytes accessed | tf_op | source)
XLA Modules:
  0.0 237.1 jit_solution(12051169796513153194)
XLA Ops:
  9.0 1.9 multiply_reduce_fusion.1
  10.9 2.1 fusion.40
  14.5 1.7 copy.17
  16.2 36.3 %all-gather.3.cloned.1.call-done = bf16[256,32,128]{2,1,0:T(8,128)(2,1)} async-done(((bf16[64,32,128]{2,1,0:T(8,128)(2,1)}), bf16[256,32,128]{2,1,0:T(8,128)(2,1)}) %all-gather.3.cloned.1.call-update) | async-done | bytes 2097168 | tf_op jit(solution)/shard_map/all_gather | solution.py:56
  52.5 3.9 %copy.18 = bf16[256,32,128]{0,1,2:T(8,128)(2,1)S(1)} copy(bf16[256,32,128]{2,1,0:T(8,128)(2,1)} %all-gather.3.cloned.1.call-done) | data formatting | bytes 4194304 | tf_op jit(solution)/shard_map/all_gather | solution.py:56
  56.4 3.3 %convert_bitcast_fusion = bf16[256,64,128]{0,1,2:T(8,128)(2,1)} fusion(bf16[64,32,128]{0,1,2:T(8,128)(2,1)S(1)} %copy.17, bf16[256,32,128]{0,1,2:T(8,128)(2,1)S(1)} %copy.18), kind=kOutput, calls=%fused_computation.24 | convolution fusion | flops 136314880 | bytes 6815744 | tf_op jit(solution)/shard_map/jkc,ikc->jic/dot_general | solution.py:58
  59.7 7.4 %copy.19 = bf16[256,64,128]{2,1,0:T(8,128)(2,1)} copy(bf16[256,64,128]{0,1,2:T(8,128)(2,1)} %convert_bitcast_fusion) | data formatting | bytes 8388608 | tf_op jit(solution)/shard_map/convert_element_type | solution.py:60
  67.1 50.0 %reduce-scatter.2.cloned.1.call-done = bf16[32,64,128]{2,1,0:T(8,128)(2,1)} async-done(((bf16[256,64,128]{2,1,0:T(8,128)(2,1)}), bf16[32,64,128]{2,1,0:T(8,128)(2,1)}) %reduce-scatter.2.cloned.1.call-update) | async-done | bytes 524304 | tf_op jit(solution)/shard_map/reduce_scatter | solution.py:57
  118.5 1.7 fusion.28
  120.2 1.6 fusion.29
  122.4 1.7 fusion.63
  126.2 1.8 convolution_convert_fusion.1
  128.1 9.1 %all_gather.11 = bf16[256,32,4]{1,2,0:T(4,128)(2,1)S(1)} all-gather(bf16[64,32,4]{1,2,0:T(4,128)(2,1)S(1)} %convolution_convert_fusion.1), channel_id=1, replica_groups=mesh['row'=4,'col'=8] {'row'}, dimensions={0}, use_global_device_ids=true | all-gather | bytes 81920 | tf_op jit(solution)/shard_map/all_gather | solution.py:78
  138.1 3.5 %all-to-all-start = ((bf16[8,2,2048]{2,1,0:T(2,128)(2,1)}), bf16[8,2,2048]{2,1,0:T(2,128)(2,1)S(1)}, u32[]{:S(2)}, u32[]{:S(2)}) async-start(bf16[8,2,2048]{2,1,0:T(2,128)(2,1)} %reshape.132), calls=%async_computation.1 | async-start | bytes 131072 | tf_op jit(solution)/shard_map/all_to_all | solution.py:79
  141.6 2.1 fusion.25
  143.7 3.1 %reshape.116 = bf16[8,8,32,4,32]{4,3,2,1,0:T(4,128)(2,1)S(1)} reshape(bf16[64,32,128]{2,1,0:T(8,128)(2,1)} %fusion.25) | data formatting | bytes 1048576 | tf_op jit(solution)/shard_map/reshape | solution.py:87
  146.9 2.2 all-to-all-done
  153.3 19.8 %all-gather.5.cloned.1.call-done = bf16[64,256,128]{2,1,0:T(8,128)(2,1)} async-done(((bf16[64,32,128]{2,1,0:T(8,128)(2,1)}), bf16[64,256,128]{2,1,0:T(8,128)(2,1)}) %all-gather.5.cloned.1.call-update) | async-done | bytes 4194320 | tf_op jit(solution)/shard_map/all_gather | solution.py:97
  173.1 4.6 %convolution_convert_fusion = bf16[64,256,256]{1,2,0:T(8,128)(2,1)S(1)} fusion(bf16[64,256,128]{2,1,0:T(8,128)(2,1)} %all-gather.5.cloned.1.call-done, bf16[128,512]{1,0:T(8,128)(2,1)} %param.15), kind=kOutput, calls=%fused_computation.23 | convolution fusion | flops 1077936128 | bytes 12648448 | tf_op jit(solution)/shard_map/dot_general | solution.py:96
  177.7 3.5 %fusion.62 = (bf16[64,256,128]{1,2,0:T(8,128)(2,1)}, bf16[64,256,128]{1,2,0:T(8,128)(2,1)}) fusion(bf16[64,256,256]{1,2,0:T(8,128)(2,1)S(1)} %convolution_convert_fusion), kind=kLoop, calls=%fused_computation.96 | loop fusion | bytes 16777216 | tf_op jit(solution)/shard_map/slice | solution.py:102
  181.2 39.1 %while.13 = (s32[]{:T(128)}, f32[8,8,4,32]{3,2,1,0:T(4,128)S(1)}, f32[8,8,32,4,32]{2,4,3,1,0:T(8,128)}, bf16[8,8,32,4,32]{4,3,2,1,0:T(4,128)(2,1)S(1)}, bf16[8,8...) while((s32[]{:T(128)}, f32[8,8,4,32]{3,2,1,0:T(4,128)S(1)}, ...), condition=%wide.region_10.11_spmd.clone, body=%wide.region_7.10_spmd.clone.sunk | while | flops 35165696 | bytes 5131381 | solution.py:30
  183.8 2.3 fusion.79
  188.8 2.3 fusion.79
  193.7 2.2 fusion.79
  198.6 2.2 fusion.79
  203.4 2.2 fusion.79
  208.3 2.2 fusion.79
  213.2 2.2 fusion.79
  218.1 2.2 fusion.79
  220.3 5.0 %broadcast_divide_fusion = f32[8,8,32,4,32]{2,4,3,1,0:T(8,128)} fusion(f32[8,8,32,4,32]{2,4,3,1,0:T(8,128)} %get-tuple-element.48, f32[8,8,32,4]{2,3,1,0:T(4,128)S(1)} %bitcast.104), kind=kLoop, calls=%fused_computation.25 | loop fusion | flops 262144 | bytes 2129920 | tf_op jit(solution)/shard_map/div | solution.py:106
  225.4 2.9 %copy.27 = f32[64,32,128]{2,1,0:T(8,128)S(1)} copy(f32[64,32,128]{1,2,0:T(8,128)} %bitcast.98) | data formatting | bytes 2097152 | tf_op jit(solution)/shard_map/reshape | solution.py:107
  228.2 2.3 convolution_add_fusion.1
  (91 shorter events, 33.3 us)
Async XLA Ops:
  6.5 4.4 %copy-start = (bf16[128,512]{1,0:T(8,128)(2,1)S(1)}, bf16[128,512]{1,0:T(8,128)(2,1)}, u32[]{:S(2)}) copy-start(bf16[128,512]{1,0:T(8,128)(2,1)} %param.12) | copy-start | bytes 393220
  6.5 45.9 %all-gather.3.cloned.1.call-start = ((), (), s32[]{:S(2)}) async-start(), calls=%async_computation.2 | async-start | bytes 2621440 | tf_op jit(solution)/shard_map/all_gather | solution.py:56
  14.4 102.7 %reduce-scatter.2.cloned.1.call-start = ((), (), s32[]{:S(2)}) async-start(), calls=%async_computation.3 | async-start | bytes 4718592 | tf_op jit(solution)/shard_map/reduce_scatter | solution.py:57
  67.1 54.9 %copy-start.3 = (bf16[128,128]{1,0:T(8,128)(2,1)S(1)}, bf16[128,128]{1,0:T(8,128)(2,1)}, u32[]{:S(2)}) copy-start(bf16[128,128]{1,0:T(8,128)(2,1)} %param.14) | copy-start | bytes 98308
  67.1 55.3 %copy-start.1 = (f32[64,32,128]{2,1,0:T(8,128)S(1)}, f32[64,32,128]{2,1,0:T(8,128)}, u32[]{:S(2)}) copy-start(f32[64,32,128]{2,1,0:T(8,128)} %param.10) | copy-start | bytes 3145732
  67.1 55.3 %copy-start.5 = (bf16[128,128]{1,0:T(8,128)(2,1)S(1)}, bf16[128,128]{1,0:T(8,128)(2,1)}, u32[]{:S(2)}) copy-start(bf16[128,128]{1,0:T(8,128)(2,1)} %param.13) | copy-start | bytes 98308
  67.1 106.0 %all-gather.5.cloned.1.call-start = ((), (), s32[]{:S(2)}) async-start(), calls=%async_computation.4 | async-start | bytes 4718592 | tf_op jit(solution)/shard_map/all_gather | solution.py:97
  122.3 3.9 %copy-start.4 = (bf16[128,4]{0,1:T(4,128)(2,1)S(1)}, bf16[128,4]{0,1:T(4,128)(2,1)}, u32[]{:S(2)}) copy-start(bf16[128,4]{0,1:T(4,128)(2,1)} %param.16) | copy-start | bytes 3076
  138.1 11.0 %all-to-all-start = ((bf16[8,2,2048]{2,1,0:T(2,128)(2,1)}), bf16[8,2,2048]{2,1,0:T(2,128)(2,1)S(1)}, u32[]{:S(2)}, u32[]{:S(2)}) async-start(bf16[8,2,2048]{2,1,0:T(2,128)(2,1)} %reshape.132), calls=%async_computation.1 | async-start | bytes 131072 | tf_op jit(solution)/shard_map/all_to_all | solution.py:79
  225.4 2.9 %copy-start.2 = (bf16[64,32,128]{2,1,0:T(8,128)(2,1)S(1)}, bf16[64,32,128]{2,1,0:T(8,128)(2,1)}, u32[]{:S(2)}) copy-start(bf16[64,32,128]{2,1,0:T(8,128)(2,1)} %multiply_convert_fusion) | copy-start | bytes 1572868
  225.4 2.9 %copy-start.6 = (bf16[128,128]{1,0:T(8,128)(2,1)S(1)}, bf16[128,128]{1,0:T(8,128)(2,1)}, u32[]{:S(2)}) copy-start(bf16[128,128]{1,0:T(8,128)(2,1)} %param.17) | copy-start | bytes 98308
Sparse Core Ops, SparseCore 0:
  14.5 37.8 all-gather.2
  67.2 49.8 reduce-scatter.1
  126.3 46.7 all-gather.4
where the time goes:
time: 239 us; the launch traced here: 237 us
  waiting for transfers between devices  108 us (45%)
  matrix products  47.5 us (20%)
  local copies, waits for them, and re-layouts  27.6 us (12%)
  other arithmetic  26.6 us (11%)
  between operations  14 us (6%)
  blocking collectives  9.12 us (4%)
  starting transfers between devices  3.61 us (2%)
    reduce_scatter x1, waiting for transfers between devices, per_device(): lax.psum_scatter(jnp.einsum('jkc,ikc->jic', right_rows, left_edges, prefe...  50 us
    all_gather x1, waiting for transfers between devices, per_device(): right_rows = lax.all_gather(right_edges, 'row', axis=0, tiled=True)  36.3 us
    all_gather x1, waiting for transfers between devices, per_device(): lax.all_gather(normed_mid, 'col', axis=1, tiled=True)  19.8 us
    dot_general x8, matrix products, one_block(): jnp.einsum('ihjk,ikhd->ijhd', expo, values.astype(jnp.float32))  17.9 us
    dot_general x8, matrix products, one_block(): jnp.einsum('ijhd,ikhd->ihjk', query, keys, preferred_element_type=jnp.flo...  11.3 us
    all_gather x1, blocking collectives, per_device(): bias_rows = lax.all_gather(bias_local, 'row', axis=0, tiled=True)  9.12 us
    convert_element_type x1, local copies, waits for them, and re-layouts, per_device(): swapped = lax.psum_scatter(jnp.einsum('jkc,ikc->jic', right_rows, left_ed...  7.38 us
    select_n x8, other arithmetic, per_device(): jnp.where(tokens < valid_length[0], 0.0, -1000000000.0).astype(jnp.float32)  5.17 us
  transfers between devices with their start and end apart: 4, of which 4 were waited for; matrix products, arithmetic and copies ran while one was open for 6% of the time, Pallas kernels for 0%

commit v1 on v0

v1 whole, which is shorter than its diff:
```python
import functools

import jax
import jax.numpy as jnp
from jax import lax
from jax.experimental import pallas as pl
from jax.experimental.pallas import tpu as pltpu
from jax.sharding import PartitionSpec as P

MESH = pl.DeviceIdType.MESH
F32 = jnp.float32
BF16 = jnp.bfloat16


def norm(values, axis):
    center = values - jnp.mean(values, axis=axis, keepdims=True)
    return center * lax.rsqrt(jnp.mean(center * center, axis=axis, keepdims=True) + 1e-05)


def swap_groups(blocks, lane, group):
    count = len(blocks)
    width = count * group
    out = []
    for b in range(count):
        total = None
        for a in range(count):
            shift = (group * (a - b)) % width
            moved = blocks[a] if shift == 0 else pltpu.roll(blocks[a], shift, 1)
            total = moved if total is None else jnp.where(lane == a, moved, total)
        out.append(total)
    return out


def kernel(
    dims,
    pair_ref, keep_ref, mask_ref, tri_in_ref, tri_gate_ref, tri_out_ref, att_in_ref, bias_w_ref,
    middle_ref, gated_ref,
    edge_f, edge_send, edge_recv, left_s, right_s, prod_send, prod_recv, prod_f,
    mid_send, mid_recv, qkv_s, gate_s, bias_f, bias_send, bias_recv, bias_full, gated_s,
    send1, recv1, send2, recv2, send3, recv3, send4, recv4, send5, recv5,
):
    nrow, ncol, rows_dev, cols_dev, width, heads = dims
    ndev = nrow * ncol
    total = ncol * cols_dev
    group = 128 // cols_dev
    tiles = rows_dev // group
    chans = width // ndev
    per = rows_dev // ncol
    head_size = width // heads
    my_row, my_col = lax.axis_index("row"), lax.axis_index("col")
    me = my_row * ncol + my_col

    def other(step):
        peer = lax.rem(me + step, ndev)
        return peer, (peer // ncol, lax.rem(peer, ncol))

    barrier = pltpu.get_barrier_semaphore()

    def greet(step, carry):
        pl.semaphore_signal(barrier, inc=1, device_id=other(step)[1], device_id_type=MESH)
        return carry

    lax.fori_loop(1, ndev, greet, 0)

    for t in range(tiles):
        rows = jnp.concatenate([pair_ref[g * tiles + t] for g in range(group)], axis=0)
        normed = norm(rows, 1).astype(BF16)
        proj = jnp.dot(normed, tri_in_ref[...], preferred_element_type=F32)
        keep = keep_ref[pl.ds(t, 1), :]
        left = jax.nn.sigmoid(proj[:, :width]) * proj[:, width : 2 * width]
        right = jax.nn.sigmoid(proj[:, 2 * width : 3 * width]) * proj[:, 3 * width :]
        edge_f[pl.ds(t, width, stride=2 * tiles), :] = jnp.transpose(left) * keep
        edge_f[pl.ds(tiles + t, width, stride=2 * tiles), :] = jnp.transpose(right) * keep
    span = chans * 2 * tiles
    for d in range(ndev):
        edge_send[d] = edge_f[pl.ds(d * span, span), :].astype(BF16)
    pl.semaphore_wait(barrier, ndev - 1)

    def exchange(source, target, sends, recvs):
        def make(step):
            peer, where = other(step)
            return pltpu.make_async_remote_copy(
                src_ref=source(peer), dst_ref=target, send_sem=sends.at[step],
                recv_sem=recvs.at[step], device_id=where, device_id_type=MESH,
            )

        def begin(step, carry):
            make(step).start()
            return carry

        def finish(step, carry):
            make(step).wait()
            return carry

        return (
            lambda: lax.fori_loop(1, ndev, begin, 0),
            lambda: lax.fori_loop(1, ndev, finish, 0),
        )

    start, wait = exchange(lambda d: edge_send.at[d], edge_recv.at[me], send1, recv1)
    start()
    edge_recv[me] = edge_send[me]
    wait()

    lane = lax.broadcasted_iota(jnp.int32, (tiles, 128), 1) // cols_dev
    for c in range(chans):
        for side, operand in ((0, left_s), (1, right_s)):
            first = (c * 2 + side) * tiles
            for r in range(nrow):
                for half in range(ncol // group):
                    blocks = [
                        edge_recv[r * ncol + half * group + a, first : first + tiles, :].astype(F32)
                        for a in range(group)
                    ]
                    for b, piece in enumerate(swap_groups(blocks, lane, cols_dev)):
                        operand[
                            pl.ds(r * rows_dev + b * tiles, tiles), pl.ds(half * 128, 128)
                        ] = piece.astype(BF16)
        products = lax.dot_general(
            left_s[...], right_s[...], (((1,), (1,)), ((), ())), preferred_element_type=F32
        )
        for r in range(nrow):
            for half in range(ncol // group):
                blocks = [
                    products[
                        r * rows_dev + a * tiles : r * rows_dev + (a + 1) * tiles,
                        half * 128 : (half + 1) * 128,
                    ]
                    for a in range(group)
                ]
                for b, piece in enumerate(swap_groups(blocks, lane, cols_dev)):
                    prod_send[
                        r * ncol + half * group + b, pl.ds(c * tiles, tiles), :
                    ] = piece.astype(BF16)

    start, wait = exchange(lambda d: prod_send.at[d], prod_recv.at[me], send2, recv2)
    start()
    prod_recv[me] = prod_send[me]
    wait()

    span = chans * tiles
    for d in range(ndev):
        prod_f[pl.ds(d * span, span), :] = prod_recv[d].astype(F32)
    for t in range(tiles):
        prods = norm(prod_f[pl.ds(t, width, stride=tiles), :], 0)
        prods = jnp.transpose(prods).astype(BF16)
        update = jnp.dot(prods, tri_out_ref[...], preferred_element_type=F32)
        rows = jnp.concatenate([pair_ref[g * tiles + t] for g in range(group)], axis=0)
        normed = norm(rows, 1).astype(BF16)
        gate = jax.nn.sigmoid(jnp.dot(normed, tri_gate_ref[...], preferred_element_type=F32))
        middle = rows + gate * update
        normed_mid = norm(middle, 1).astype(BF16)
        for g in range(group):
            i = g * tiles + t
            middle_ref[i] = middle[g * cols_dev : (g + 1) * cols_dev]
            mid_send[i // per, i % per] = normed_mid[g * cols_dev : (g + 1) * cols_dev]

    mine = pl.ds(pl.multiple_of(my_col * cols_dev, cols_dev), cols_dev)

    def mid_copy(step):
        peer = lax.rem(my_col + step, ncol)
        return pltpu.make_async_remote_copy(
            src_ref=mid_send.at[peer], dst_ref=mid_recv.at[:, mine, :], send_sem=send3.at[step],
            recv_sem=recv3.at[step], device_id=(my_row, peer), device_id_type=MESH,
        )

    for step in range(1, ncol):
        mid_copy(step).start()
    mid_recv[:, mine, :] = mid_send[my_col]
    for step in range(1, ncol):
        mid_copy(step).wait()

    for i in range(per):
        own = lax.dot_general(
            bias_w_ref[...], mid_recv[i], (((1,), (1,)), ((), ())), preferred_element_type=F32
        )
        for h in range(heads):
            bias_f[pl.ds(h * per + i, 1), :] = own[h : h + 1]
    bias_send[...] = bias_f[...].astype(BF16)
    start, wait = exchange(lambda d: bias_send, bias_recv.at[me], send4, recv4)
    start()
    bias_recv[me] = bias_send[...]
    for i in range(per):
        proj = jnp.dot(mid_recv[i], att_in_ref[...], preferred_element_type=F32)
        qkv_s[i, :, :width] = (proj[:, :width] * head_size ** (-0.5)).astype(BF16)
        qkv_s[i, :, width : 3 * width] = proj[:, width : 3 * width].astype(BF16)
        gate_s[i] = jax.nn.sigmoid(proj[:, 3 * width :])
    wait()
    mask = mask_ref[...]
    for d in range(ndev):
        piece = bias_recv[d].astype(F32) + mask
        for h in range(heads):
            bias_full[h, pl.ds(d * per, per), :] = piece[h * per : (h + 1) * per]

    head = lax.broadcasted_iota(jnp.int32, (total, width), 1) // head_size

    def home_copy(i, step):
        peer = lax.rem(my_col + step, ncol)
        theirs = pl.ds(pl.multiple_of(peer * cols_dev, cols_dev), cols_dev)
        return pltpu.make_async_remote_copy(
            src_ref=gated_s.at[i, theirs, :], dst_ref=gated_ref.at[my_col * per + i],
            send_sem=send5.at[i, step], recv_sem=recv5.at[i, step],
            device_id=(my_row, peer), device_id_type=MESH,
        )

    def attend(i, carry):
        query = qkv_s[i, :, :width]
        keys = qkv_s[i, :, width : 2 * width]
        values = jnp.concatenate(
            [qkv_s[i, :, 2 * width : 3 * width], jnp.ones((total, width), BF16)], axis=1
        )
        joined = jnp.zeros((total, width), F32)
        for h in range(heads):
            scores = lax.dot_general(
                jnp.where(head == h, query, jnp.zeros_like(query)), keys,
                (((1,), (1,)), ((), ())), preferred_element_type=F32,
            )
            scores = scores + bias_full[h]
            expo = jnp.exp(scores - jnp.max(scores, axis=1, keepdims=True)).astype(BF16)
            both = jnp.dot(expo, values, preferred_element_type=F32)
            joined = jnp.where(head == h, both[:, :width] / both[:, width:], joined)
        gated_s[i] = (gate_s[i] * joined).astype(BF16)
        for step in range(1, ncol):
            home_copy(i, step).start()
        gated_ref[my_col * per + i] = gated_s[i, mine, :]
        return carry

    lax.fori_loop(0, per, attend, 0)

    def finish(i, carry):
        for step in range(1, ncol):
            home_copy(i, step).wait()
        return carry

    lax.fori_loop(0, per, finish, 0)


def per_device(pair, valid_length, tri_in, tri_gate, tri_out, att_in, att_bias, att_out):
    rows_dev, cols_dev, width = pair.shape
    heads = att_bias.shape[1]
    nrow, ncol = lax.axis_size("row"), lax.axis_size("col")
    ndev = nrow * ncol
    total = ncol * cols_dev
    group = 128 // cols_dev
    tiles = rows_dev // group
    chans = width // ndev
    per = rows_dev // ncol
    row_ids = lax.axis_index("row") * rows_dev + jnp.arange(rows_dev)
    col_ids = lax.axis_index("col") * cols_dev + jnp.arange(cols_dev)
    keep = ((row_ids < valid_length[0])[:, None] & (col_ids < valid_length[0])[None, :]).astype(F32)
    keep = keep.reshape(group, tiles, cols_dev).transpose(1, 0, 2).reshape(tiles, 128)
    mask = jnp.where(jnp.arange(total) < valid_length[0], 0.0, -1000000000.0).astype(F32)[None]
    bias_w = jnp.pad(att_bias.T, ((0, 16 - heads), (0, 0)))
    vmem = pl.BlockSpec(memory_space=pltpu.VMEM)
    dma = pltpu.SemaphoreType.DMA
    middle, gated = pl.pallas_call(
        functools.partial(kernel, (nrow, ncol, rows_dev, cols_dev, width, heads)),
        out_shape=(
            jax.ShapeDtypeStruct((rows_dev, cols_dev, width), F32),
            jax.ShapeDtypeStruct((rows_dev, cols_dev, width), BF16),
        ),
        in_specs=[vmem] * 8,
        out_specs=(vmem, vmem),
        scratch_shapes=[
            pltpu.VMEM((width * 2 * tiles, 128), F32),
            pltpu.VMEM((ndev, chans * 2 * tiles, 128), BF16),
            pltpu.VMEM((ndev, chans * 2 * tiles, 128), BF16),
            pltpu.VMEM((total, total), BF16),
            pltpu.VMEM((total, total), BF16),
            pltpu.VMEM((ndev, chans * tiles, 128), BF16),
            pltpu.VMEM((ndev, chans * tiles, 128), BF16),
            pltpu.VMEM((width * tiles, 128), F32),
            pltpu.VMEM((ncol, per, cols_dev, width), BF16),
            pltpu.VMEM((per, total, width), BF16),
            pltpu.VMEM((per, total, 3 * width), BF16),
            pltpu.VMEM((per, total, width), F32),
            pltpu.VMEM((heads * per, total), F32),
            pltpu.VMEM((heads * per, total), BF16),
            pltpu.VMEM((ndev, heads * per, total), BF16),
            pltpu.VMEM((heads, total, total), F32),
            pltpu.VMEM((per, total, width), BF16),
            dma((ndev,)), dma((ndev,)), dma((ndev,)), dma((ndev,)),
            dma((ncol,)), dma((ncol,)), dma((ndev,)), dma((ndev,)),
            dma((per, ncol)), dma((per, ncol)),
        ],
        compiler_params=pltpu.CompilerParams(
            collective_id=0, has_side_effects=True, vmem_limit_bytes=56 * 1024 * 1024
        ),
    )(pair, keep, mask, tri_in, tri_gate, tri_out, att_in, bias_w)
    return middle + jnp.dot(gated, att_out, preferred_element_type=F32)


def solution(mesh):
    placed = (P("row", "col", None), P(), P(), P(), P(), P(), P(), P())
    return jax.shard_map(
        per_device, mesh=mesh, in_specs=placed, out_specs=P("row", "col", None), check_vma=False
    )
```

time: 239 us -> 102 us (0.43)
  waiting for transfers between devices: 108 us -> 0 us
  Pallas kernels: 0 us -> 95.5 us
  matrix products: 47.5 us -> 2.65 us
  local copies, waits for them, and re-layouts: 27.6 us -> 1.53 us
  other arithmetic: 26.6 us -> 1.22 us
  between operations: 14 us -> 0.7 us
  blocking collectives: 9.12 us -> 0 us
  starting transfers between devices: 3.61 us -> 0 us
    pallas_call x0 -> x1, Pallas kernels: none -> 95.5 us  [per_device(): pl.pallas_call(functools.partial(kernel, (nrow, ncol, rows_dev, cols_dev,...]
    all_gather x2 -> x0, waiting for transfers between devices: 56.1 us -> none  [the longest x1 36.3 us: per_device(): right_rows = lax.all_gather(right_edges, 'row', axis=0, tiled=True)]
    reduce_scatter x1 -> x0, waiting for transfers between devices: 50 us -> none  [per_device(): lax.psum_scatter(jnp.einsum('jkc,ikc->jic', right_rows, left_edges, prefe...]
    dot_general x24 -> x1, matrix products: 47.5 us -> 2.65 us  [per_device(): return middle + jnp.dot(gated, att_out, preferred_element_type=F32)]
    reduce_sum x13 -> x0, other arithmetic: 10.4 us -> none  [the longest x3 4.18 us: layer_norm(): jnp.mean(center * center, axis=-1, keepdims=True) + 1e-05]
    all_gather x1 -> x0, blocking collectives: 9.12 us -> none  [per_device(): bias_rows = lax.all_gather(bias_local, 'row', axis=0, tiled=True)]
    convert_element_type x2 -> x0, local copies, waits for them, and re-layouts: 9.07 us -> none  [the longest x1 7.38 us: per_device(): swapped = lax.psum_scatter(jnp.einsum('jkc,ikc->jic', right_rows, left_ed...]
    reshape x2 -> x0, local copies, waits for them, and re-layouts: 5.96 us -> none  [the longest x1 3.11 us: per_device(): query_blocks = query.reshape(nblocks, 8, cols_dev, heads, head_size)]
  transfers between devices with their start and end apart: 4 -> 0, of which waited for: 4 -> 0; matrix products, arithmetic and copies ran while one was open for 6% -> 0% of each run, Pallas kernels for 0% -> 0%
where the time goes in v1:
time: 102 us
  Pallas kernels  95.5 us (94%)
  matrix products  2.65 us (3%)
  local copies, waits for them, and re-layouts  1.53 us (2%)
  other arithmetic  1.22 us (1%)
    pallas_call x1, Pallas kernels, per_device(): pl.pallas_call(functools.partial(kernel, (nrow, ncol, rows_dev, cols_dev,...  95.5 us
    dot_general x1, matrix products, per_device(): return middle + jnp.dot(gated, att_out, preferred_element_type=F32)  2.65 us

profile of v1, /device:TPU:0, one launch (start us, length us, event | category | flops | bytes accessed | tf_op | source)
XLA Modules:
  0.0 101.6 jit_solution(17999242359520458497)
XLA Ops:
  0.0 0.0 copy-start
  0.7 0.1 and.27
  0.8 0.6 compare_select_fusion.mask_ref
  1.4 0.0 copy-start.1
  1.4 0.7 copy-done.1
  2.0 0.6 pad.4.bias_w_ref
  2.6 0.1 and.24
  2.7 0.1 and.25
  2.8 0.6 and_convert_fusion.keep_ref
  3.4 95.5 %shard_map.82 = (f32[64,32,128]{2,1,0:T(8,128)}, bf16[64,32,128]{2,1,0:T(8,128)(2,1)}) custom-call(f32[64,32,128]{2,1,0:T(8,128)} %pair_ref.1, f32[16,128]{1,0:T(8,128)} %and_convert_fusion.keep_ref, f32[1,256]{1,0:T(1,128)} %compare_select_fusion.mask_ref, bf16[128,512]{1,0:T(8,128)(2,1)} %tri_in_ref.1, bf16[128,128]{1,0:T(8,128)(2,1)} %tri_gate_ref.1, ...), custom_call_target="tpu_custom_call" | custom-call | tf_op jit(solution)/shard_map/pallas_call | solution.py:256
  99.0 0.0 copy-done
  99.0 2.6 %convolution_add_fusion = f32[64,32,128]{2,1,0:T(8,128)} fusion(f32[64,32,128]{2,1,0:T(8,128)} %get-tuple-element.7, bf16[64,32,128]{2,1,0:T(8,128)(2,1)} %get-tuple-element.8, bf16[128,128]{1,0:T(8,128)(2,1)S(1)} %copy-done), kind=kOutput, calls=%fused_computation | convolution fusion | flops 67371008 | bytes 2654208 | tf_op jit(solution)/shard_map/dot_general | solution.py:290
  (3 shorter events, 0.0 us)
Async XLA Ops:
  0.0 99.0 %copy-start = (bf16[128,128]{1,0:T(8,128)(2,1)S(1)}, bf16[128,128]{1,0:T(8,128)(2,1)}, u32[]{:S(2)}) copy-start(bf16[128,128]{1,0:T(8,128)(2,1)} %param.15) | copy-start | bytes 98308
  1.4 0.7 copy-start.1

commit v2 on v1

v2 whole, which is shorter than its diff:
```python
import functools

import jax
import jax.numpy as jnp
from jax import lax
from jax.experimental import pallas as pl
from jax.experimental.pallas import tpu as pltpu
from jax.sharding import PartitionSpec as P

MESH = pl.DeviceIdType.MESH
F32 = jnp.float32
BF16 = jnp.bfloat16


def norm(values, axis):
    center = values - jnp.mean(values, axis=axis, keepdims=True)
    return center * lax.rsqrt(jnp.mean(center * center, axis=axis, keepdims=True) + 1e-05)


def swap_groups(blocks, lane, group):
    count = len(blocks)
    width = count * group
    out = []
    for b in range(count):
        total = None
        for a in range(count):
            shift = (group * (a - b)) % width
            moved = blocks[a] if shift == 0 else pltpu.roll(blocks[a], shift, 1)
            total = moved if total is None else jnp.where(lane == a, moved, total)
        out.append(total)
    return out


def kernel(
    dims,
    valid_ref, pair_ref, tri_in_ref, tri_gate_ref, tri_out_ref, att_in_ref, bias_w_ref, att_out_ref,
    out_ref,
    normed_s, edge_f, left_send, right_send, left_recv, right_recv, left_s, right_s,
    prod_send, prod_recv, prod_f, tri_gate_s, mid_send, mid_recv, qkv_s, gate_s,
    bias_f, bias_send, bias_recv, bias_full, gated_s, gated_recv,
    send_l, recv_l, send_r, recv_r, send_p, recv_p, send_m, recv_m, send_b, recv_b, send_c, recv_c,
    send_g, recv_g,
):
    nrow, ncol, rows_dev, cols_dev, width, heads = dims
    ndev = nrow * ncol
    total = ncol * cols_dev
    group = 128 // cols_dev
    tiles = rows_dev // group
    chans = width // ndev
    parts = 2 if chans % 2 == 0 else 1
    each = chans // parts
    per = rows_dev // ncol
    head_size = width // heads
    my_row, my_col = lax.axis_index("row"), lax.axis_index("col")
    me = my_row * ncol + my_col
    valid = valid_ref[0]

    def other(step):
        peer = lax.rem(me + step, ndev)
        return peer, (peer // ncol, lax.rem(peer, ncol))

    def loop(count, act):
        def run(step, carry):
            act(step)
            return carry

        lax.fori_loop(1, count, run, 0)

    barrier = pltpu.get_barrier_semaphore()
    loop(
        ndev,
        lambda step: pl.semaphore_signal(
            barrier, inc=1, device_id=other(step)[1], device_id_type=MESH
        ),
    )

    lanes = lax.broadcasted_iota(jnp.int32, (1, 128), 1)
    lane_col = my_col * cols_dev + lanes % cols_dev
    lane_row = my_row * rows_dev + (lanes // cols_dev) * tiles

    def edges(side):
        first = 2 * side * width
        for t in range(tiles):
            if side == 0:
                rows = jnp.concatenate([pair_ref[g * tiles + t] for g in range(group)], axis=0)
                normed_s[t] = norm(rows, 1).astype(BF16)
            proj = jnp.dot(
                normed_s[t], tri_in_ref[:, first : first + 2 * width], preferred_element_type=F32
            )
            keep = jnp.where((lane_row + t < valid) & (lane_col < valid), 1.0, 0.0)
            edge = jax.nn.sigmoid(proj[:, :width]) * proj[:, width:]
            edge_f[side, pl.ds(t, width, stride=tiles), :] = jnp.transpose(edge) * keep

    def pack(side, target):
        for c in range(chans):
            target[c] = edge_f[side, pl.ds(c * ndev * tiles, ndev * tiles), :].astype(BF16)

    def share(peer):
        return pl.ds(pl.multiple_of(peer * tiles, tiles), tiles)

    def left_copy(step):
        peer, where = other(step)
        return pltpu.make_async_remote_copy(
            src_ref=left_send.at[:, share(peer), :], dst_ref=left_recv.at[me],
            send_sem=send_l.at[step], recv_sem=recv_l.at[step],
            device_id=where, device_id_type=MESH,
        )

    def right_copy(part, step):
        peer, where = other(step)
        some = pl.ds(part * each, each)
        return pltpu.make_async_remote_copy(
            src_ref=right_send.at[some, share(peer), :], dst_ref=right_recv.at[me, some],
            send_sem=send_r.at[part, step], recv_sem=recv_r.at[part, step],
            device_id=where, device_id_type=MESH,
        )

    edges(0)
    pack(0, left_send)
    pl.semaphore_wait(barrier, ndev - 1)
    loop(ndev, lambda step: left_copy(step).start())
    edges(1)
    pack(1, right_send)
    for part in range(parts):
        loop(ndev, lambda step: right_copy(part, step).start())
    left_recv[me] = left_send[:, share(me), :]
    right_recv[me] = right_send[:, share(me), :]
    for t in range(tiles):
        tri_gate_s[t] = jax.nn.sigmoid(
            jnp.dot(normed_s[t], tri_gate_ref[...], preferred_element_type=F32)
        )
    loop(ndev, lambda step: left_copy(step).wait())

    lane = lax.broadcasted_iota(jnp.int32, (tiles, 128), 1) // cols_dev

    def spread(c, source, operand):
        for r in range(nrow):
            for half in range(ncol // group):
                blocks = [
                    source[r * ncol + half * group + a, c].astype(F32) for a in range(group)
                ]
                for b, piece in enumerate(swap_groups(blocks, lane, cols_dev)):
                    operand[
                        pl.ds(r * rows_dev + b * tiles, tiles), pl.ds(half * 128, 128)
                    ] = piece.astype(BF16)

    def prod_copy(part, step):
        peer, where = other(step)
        some = pl.ds(part * each, each)
        return pltpu.make_async_remote_copy(
            src_ref=prod_send.at[peer, some], dst_ref=prod_recv.at[me, some],
            send_sem=send_p.at[part, step], recv_sem=recv_p.at[part, step],
            device_id=where, device_id_type=MESH,
        )

    for c in range(chans):
        spread(c, left_recv, left_s.at[c])
    for part in range(parts):
        loop(ndev, lambda step: right_copy(part, step).wait())
        for c in range(part * each, (part + 1) * each):
            spread(c, right_recv, right_s.at[c])
            products = lax.dot_general(
                left_s[c], right_s[c], (((1,), (1,)), ((), ())), preferred_element_type=F32
            )
            for r in range(nrow):
                for half in range(ncol // group):
                    blocks = [
                        products[
                            r * rows_dev + a * tiles : r * rows_dev + (a + 1) * tiles,
                            half * 128 : (half + 1) * 128,
                        ]
                        for a in range(group)
                    ]
                    for b, piece in enumerate(swap_groups(blocks, lane, cols_dev)):
                        prod_send[r * ncol + half * group + b, c] = piece.astype(BF16)
        loop(ndev, lambda step: prod_copy(part, step).start())
    prod_recv[me] = prod_send[me]

    for part in range(parts):
        loop(ndev, lambda step: prod_copy(part, step).wait())
        for c in range(part * each, (part + 1) * each):
            for d in range(ndev):
                prod_f[pl.ds((c * ndev + d) * tiles, tiles), :] = prod_recv[d, c].astype(F32)

    def strip(peer):
        return pl.ds(pl.multiple_of(peer * cols_dev, cols_dev), cols_dev)

    def mid_copy(i, step):
        peer = lax.rem(my_col + step, ncol)
        return pltpu.make_async_remote_copy(
            src_ref=mid_send.at[i, peer], dst_ref=mid_recv.at[i, strip(my_col), :],
            send_sem=send_m.at[i, step], recv_sem=recv_m.at[i, step],
            device_id=(my_row, peer), device_id_type=MESH,
        )

    for i in range(per):
        for t in range(i, tiles, per):
            prods = norm(prod_f[pl.ds(t, width, stride=tiles), :], 0)
            prods = jnp.transpose(prods).astype(BF16)
            update = jnp.dot(prods, tri_out_ref[...], preferred_element_type=F32)
            rows = jnp.concatenate([pair_ref[g * tiles + t] for g in range(group)], axis=0)
            middle = rows + tri_gate_s[t] * update
            normed_mid = norm(middle, 1).astype(BF16)
            for g in range(group):
                row = g * tiles + t
                out_ref[row] = middle[g * cols_dev : (g + 1) * cols_dev]
                mid_send[i, row // per] = normed_mid[g * cols_dev : (g + 1) * cols_dev]
        for step in range(1, ncol):
            mid_copy(i, step).start()
        mid_recv[i, strip(my_col), :] = mid_send[i, my_col]

    for i in range(per):
        for step in range(1, ncol):
            mid_copy(i, step).wait()
        own = lax.dot_general(
            bias_w_ref[...], mid_recv[i], (((0,), (1,)), ((), ())), preferred_element_type=F32
        )
        for h in range(heads):
            bias_f[pl.ds(h * per + i, 1), :] = own[h : h + 1]
        if i < per - 1:
            project(i, mid_recv, att_in_ref, qkv_s, gate_s, width, head_size)
    bias_send[...] = bias_f[...].astype(BF16)

    side = lax.rem(my_col, 2)
    mine = me // 2

    def bias_copy(step):
        peer = 2 * lax.rem(mine + step, ndev // 2) + side
        return pltpu.make_async_remote_copy(
            src_ref=bias_send, dst_ref=bias_recv.at[side, mine],
            send_sem=send_b.at[step], recv_sem=recv_b.at[step],
            device_id=(peer // ncol, lax.rem(peer, ncol)), device_id_type=MESH,
        )

    loop(ndev // 2, lambda step: bias_copy(step).start())
    bias_recv[side, mine] = bias_send[...]
    project(per - 1, mid_recv, att_in_ref, qkv_s, gate_s, width, head_size)
    loop(ndev // 2, lambda step: bias_copy(step).wait())
    hand = pltpu.make_async_remote_copy(
        src_ref=bias_recv.at[side], dst_ref=bias_recv.at[side],
        send_sem=send_c, recv_sem=recv_c,
        device_id=(my_row, my_col + 1 - 2 * side), device_id_type=MESH,
    )
    hand.start()
    hand.wait()
    tokens = lax.broadcasted_iota(jnp.int32, (1, total), 1)
    mask = jnp.where(tokens < valid, 0.0, -1000000000.0)
    for d in range(ndev):
        piece = bias_recv[d % 2, d // 2].astype(F32) + mask
        for h in range(heads):
            bias_full[h, pl.ds(d * per, per), :] = piece[h * per : (h + 1) * per]

    block = 128
    head = lax.broadcasted_iota(jnp.int32, (block, width), 1) // head_size

    def home_copy(i, step):
        peer = lax.rem(my_col + step, ncol)
        return pltpu.make_async_remote_copy(
            src_ref=gated_s.at[i, strip(peer), :], dst_ref=gated_recv.at[i, strip(my_col), :],
            send_sem=send_g.at[i, step], recv_sem=recv_g.at[i, step],
            device_id=(my_row, peer), device_id_type=MESH,
        )

    def attend(i, carry):
        keys = qkv_s[i, :, width : 2 * width]
        values = jnp.concatenate(
            [qkv_s[i, :, 2 * width : 3 * width], jnp.ones((total, width), BF16)], axis=1
        )
        for first in range(0, total, block):
            query = qkv_s[i, first : first + block, :width]
            top = jnp.zeros((block, width), F32)
            bottom = jnp.ones((block, width), F32)
            for h in range(heads):
                scores = lax.dot_general(
                    jnp.where(head == h, query, jnp.zeros_like(query)), keys,
                    (((1,), (1,)), ((), ())), preferred_element_type=F32,
                )
                scores = scores + bias_full[h, first : first + block, :]
                expo = jnp.exp(scores - jnp.max(scores, axis=1, keepdims=True)).astype(BF16)
                both = jnp.dot(expo, values, preferred_element_type=F32)
                top = jnp.where(head == h, both[:, :width], top)
                bottom = jnp.where(head == h, both[:, width:], bottom)
            gated_s[i, first : first + block, :] = (
                gate_s[i, first : first + block, :] * top / bottom
            ).astype(BF16)
        for step in range(1, ncol):
            home_copy(i, step).start()
        gated_recv[i, strip(my_col), :] = gated_s[i, strip(my_col), :]
        return carry

    lax.fori_loop(0, per, attend, 0)

    def finish(i, carry):
        for step in range(1, ncol):
            home_copy(i, step).wait()
        added = jnp.dot(gated_recv[i], att_out_ref[...], preferred_element_type=F32)
        for q in range(ncol):
            out_ref[q * per + i] += added[q * cols_dev : (q + 1) * cols_dev]
        return carry

    lax.fori_loop(0, per, finish, 0)


def project(i, mid_recv, att_in_ref, qkv_s, gate_s, width, head_size):
    proj = jnp.dot(mid_recv[i], att_in_ref[...], preferred_element_type=F32)
    qkv_s[i, :, :width] = (proj[:, :width] * head_size ** (-0.5)).astype(BF16)
    qkv_s[i, :, width : 3 * width] = proj[:, width : 3 * width].astype(BF16)
    gate_s[i] = jax.nn.sigmoid(proj[:, 3 * width :])


def per_device(pair, valid_length, tri_in, tri_gate, tri_out, att_in, att_bias, att_out):
    rows_dev, cols_dev, width = pair.shape
    heads = att_bias.shape[1]
    nrow, ncol = lax.axis_size("row"), lax.axis_size("col")
    ndev = nrow * ncol
    total = ncol * cols_dev
    tiles = rows_dev // (128 // cols_dev)
    chans = width // ndev
    parts = 2 if chans % 2 == 0 else 1
    per = rows_dev // ncol
    vmem = pl.BlockSpec(memory_space=pltpu.VMEM)
    sems = lambda *shape: [pltpu.SemaphoreType.DMA(shape)] * 2
    held = lambda dtype, *shape: pltpu.VMEM(shape, dtype)
    return pl.pallas_call(
        functools.partial(kernel, (nrow, ncol, rows_dev, cols_dev, width, heads)),
        out_shape=jax.ShapeDtypeStruct((rows_dev, cols_dev, width), F32),
        in_specs=[pl.BlockSpec(memory_space=pltpu.SMEM)] + [vmem] * 7,
        out_specs=vmem,
        scratch_shapes=[
            held(BF16, tiles, 128, width),
            held(F32, 2, width * tiles, 128),
            held(BF16, chans, ndev * tiles, 128),
            held(BF16, chans, ndev * tiles, 128),
            held(BF16, ndev, chans, tiles, 128),
            held(BF16, ndev, chans, tiles, 128),
            held(BF16, chans, total, total),
            held(BF16, chans, total, total),
            held(BF16, ndev, chans, tiles, 128),
            held(BF16, ndev, chans, tiles, 128),
            held(F32, width * tiles, 128),
            held(F32, tiles, 128, width),
            held(BF16, per, ncol, cols_dev, width),
            held(BF16, per, total, width),
            held(BF16, per, total, 3 * width),
            held(F32, per, total, width),
            held(F32, heads * per, total),
            held(BF16, heads * per, total),
            held(BF16, 2, ndev // 2, heads * per, total),
            held(F32, heads, total, total),
            held(BF16, per, total, width),
            held(BF16, per, total, width),
            *sems(ndev), *sems(parts, ndev), *sems(parts, ndev), *sems(per, ncol), *sems(ndev // 2),
            pltpu.SemaphoreType.DMA, pltpu.SemaphoreType.DMA,
            *sems(per, ncol),
        ],
        compiler_params=pltpu.CompilerParams(
            collective_id=0, has_side_effects=True, vmem_limit_bytes=56 * 1024 * 1024
        ),
    )(valid_length, pair, tri_in, tri_gate, tri_out, att_in, att_bias, att_out)


def solution(mesh):
    placed = (P("row", "col", None), P(), P(), P(), P(), P(), P(), P())
    return jax.shard_map(
        per_device, mesh=mesh, in_specs=placed, out_specs=P("row", "col", None), check_vma=False
    )
```

time: 102 us -> 91.9 us (0.901)
  Pallas kernels: 95.5 us -> 88 us
  matrix products: 2.65 us -> 0 us
  local copies, waits for them, and re-layouts: 1.53 us -> 3.01 us
  other arithmetic: 1.22 us -> 0 us
    pallas_call x1, Pallas kernels: 95.5 us -> 88 us  [per_device(): pl.pallas_call(functools.partial(kernel, (nrow, ncol, rows_dev, cols_dev,...]
    dot_general x1 -> x0, matrix products: 2.65 us -> none  [per_device(): return middle + jnp.dot(gated, att_out, preferred_element_type=F32)]
    unnamed x4, local copies, waits for them, and re-layouts: 0.67 us -> 3.01 us
where the time goes in v2:
time: 91.9 us; the launch traced here: 91.7 us
  Pallas kernels  88 us (96%)
  local copies, waits for them, and re-layouts  3.01 us (3%)
    pallas_call x1, Pallas kernels, per_device(): pl.pallas_call(functools.partial(kernel, (nrow, ncol, rows_dev, cols_dev,...  88 us
    unnamed x4, local copies, waits for them, and re-layouts  3.01 us

profile of v2, /device:TPU:0, one launch (start us, length us, event | category | flops | bytes accessed | tf_op | source)
XLA Modules:
  0.0 91.7 jit_solution(9363406197625144604)
XLA Ops:
  0.0 0.0 copy-start
  0.7 0.0 copy-done
  0.7 0.7 copy.9.bias_w_ref
  1.4 88.0 %shard_map.82 = f32[64,32,128]{2,1,0:T(8,128)} custom-call(s32[1]{0:T(128)S(6)} %copy.11.valid_ref, f32[64,32,128]{2,1,0:T(8,128)} %pair_ref.1, bf16[128,512]{1,0:T(8,128)(2,1)} %tri_in_ref.1, bf16[128,128]{1,0:T(8,128)(2,1)} %tri_gate_ref.1, bf16[128,128]{1,0:T(8,128)(2,1)} %tri_out_ref.1, bf16[128,512]{1,0:T(8,128)(2,1)} %att_in_ref.1, ...), custom_call_target="tpu_custom_call" | custom-call | tf_op jit(solution)/shard_map/pallas_call | solution.py:324
  89.4 2.3 %copy.12 = f32[64,32,128]{2,1,0:T(8,128)} copy(f32[64,32,128]{2,1,0:T(8,128)} %shard_map.82) | data formatting | bytes 2097152
Async XLA Ops:
  0.0 0.7 copy-start

commit v3 on v2

--- a/solution.py
+++ b/solution.py
@@ -213,7 +213,7 @@
         for step in range(1, ncol):
             mid_copy(i, step).wait()
         own = lax.dot_general(
-            bias_w_ref[...], mid_recv[i], (((0,), (1,)), ((), ())), preferred_element_type=F32
+            bias_w_ref[...], mid_recv[i], (((1,), (1,)), ((), ())), preferred_element_type=F32
         )
         for h in range(heads):
             bias_f[pl.ds(h * per + i, 1), :] = own[h : h + 1]
@@ -356,7 +356,7 @@
         compiler_params=pltpu.CompilerParams(
             collective_id=0, has_side_effects=True, vmem_limit_bytes=56 * 1024 * 1024
         ),
-    )(valid_length, pair, tri_in, tri_gate, tri_out, att_in, att_bias, att_out)
+    )(valid_length, pair, tri_in, tri_gate, tri_out, att_in, att_bias.T, att_out)
 
 
 def solution(mesh):

time: 91.9 us -> 91.1 us (level)
    unnamed x4 -> x1, local copies, waits for them, and re-layouts: 3.01 us -> 2.26 us
where the time goes in v3:
time: 91.1 us; the launch traced here: 90.9 us
  Pallas kernels  88 us (97%)
  local copies, waits for them, and re-layouts  2.26 us (2%)
    pallas_call x1, Pallas kernels, per_device(): pl.pallas_call(functools.partial(kernel, (nrow, ncol, rows_dev, cols_dev,...  88 us
    unnamed x1, local copies, waits for them, and re-layouts  2.26 us

profile of v3, /device:TPU:0, one launch (start us, length us, event | category | flops | bytes accessed | tf_op | source)
XLA Modules:
  0.0 90.9 jit_solution(5414853418191989328)
XLA Ops:
  0.7 88.0 %shard_map.82 = f32[64,32,128]{2,1,0:T(8,128)} custom-call(s32[1]{0:T(128)S(6)} %copy.10.valid_ref, f32[64,32,128]{2,1,0:T(8,128)} %pair_ref.1, bf16[128,512]{1,0:T(8,128)(2,1)} %tri_in_ref.1, bf16[128,128]{1,0:T(8,128)(2,1)} %tri_gate_ref.1, bf16[128,128]{1,0:T(8,128)(2,1)} %tri_out_ref.1, bf16[128,512]{1,0:T(8,128)(2,1)} %att_in_ref.1, ...), custom_call_target="tpu_custom_call" | custom-call | tf_op jit(solution)/shard_map/pallas_call | solution.py:324
  88.7 2.3 %copy.11 = f32[64,32,128]{2,1,0:T(8,128)} copy(f32[64,32,128]{2,1,0:T(8,128)} %shard_map.82) | data formatting | bytes 2097152
